TPU v7x, 32 devices: a whole 2x2x4 slice. The times are simulated.
32 devices in a mesh: clip: 2 (over y), rows: 8 (over z, x), tm: 2 (over core).
Axes of the slice: x: 2, y: 2, z: 4, core: 2. Of those that a mesh axis runs over, the one named last changes fastest.
Arguments:
- latent: bfloat16 [8, 8, 64, 192], P(('clip', 'tm'), 'rows'), parts along dimension 0, may hold values from -18 to 18
- gain_first: bfloat16 [192], replicated, may hold values from 0.099609375 to 1.8984375
- conv_first: bfloat16 [3, 3, 3, 192, 192], replicated, may hold values from -0.078125 to 0.078125
- gain_second: bfloat16 [192], replicated, may hold values from 0.099609375 to 1.8984375
- conv_second: bfloat16 [3, 3, 3, 192, 192], replicated, may hold values from -0.078125 to 0.078125
- conv_up: bfloat16 [3, 3, 96, 192], replicated, may hold values from -0.15625 to 0.15625
Outputs:
- decoded: bfloat16 [8, 16, 96, 128], P(('clip', 'tm'), 'rows'), parts along dimension 0
- peaks: float32 [6, 192], P('clip'), parts along dimension 0
There are 2 independent parts, one for each index of `clip`. A program takes and returns all parts, laid end to end along the dimension named above; an argument that names none is the same for every part. Nothing has to cross between parts.
All inputs are finite; a program needn't handle non-finite values.
Results may differ from a plain program's by a relative error of at most 0.0085.
Values may be sent and summed in bfloat16 or wider, within the bound.
A program may use at most 64 MiB of HBM per device.

v0:
```python
import functools

import jax
import jax.numpy as jnp
from jax import lax
from jax.experimental import pallas as pl
from jax.experimental.pallas import tpu as pltpu
from jax.sharding import PartitionSpec as P

MESH = pl.DeviceIdType.MESH
BF16 = jnp.bfloat16
F32 = jnp.float32
REACH = 2


def normed_silu(values, gain):
    scale = lax.rsqrt(jnp.mean(values * values, axis=-1, keepdims=True) + 1e-06)
    u = values * scale * gain
    return (u / (1.0 + jnp.exp(-u))).astype(BF16)


def peak_of(values):
    return jnp.max(jnp.abs(values.astype(F32)), axis=0, keepdims=True)


def dot(a, b):
    return jnp.dot(a, b, preferred_element_type=F32)


def dot_nt(a, b):
    return lax.dot_general(a, b, (((1,), (1,)), ((), ())), preferred_element_type=F32)


def taps_part(buf, weights, time_taps, frames, rows_out, cols):
    depth = buf.shape[-1]
    pixels = frames * rows_out * cols
    pairs = [(i, j) for i in time_taps for j in range(3)]
    lhs = jnp.concatenate(
        [
            buf[i : i + frames, j * cols : (j + rows_out) * cols, :].reshape(pixels, depth)
            for i, j in pairs
        ],
        axis=1,
    )
    return [
        dot(lhs, jnp.concatenate([weights[(i * 3 + j) * 3 + k] for i, j in pairs], axis=0))
        for k in range(3)
    ]


def shifted_sum(parts, more, cols):
    parts = [a + b for a, b in zip(parts, more)]
    pixels = parts[0].shape[0]
    col = lax.rem(lax.broadcasted_iota(jnp.int32, parts[0].shape, 0), cols)
    left = jnp.where(col == 0, 0.0, pltpu.roll(parts[0], 1, 0))
    right = jnp.where(col == cols - 1, 0.0, pltpu.roll(parts[2], pixels - 1, 0))
    return left + parts[1] + right


def finish(dec_in, peaks_in, dec_out, peaks_out, sem):
    copies = [
        pltpu.make_async_copy(dec_in, dec_out, sem.at[0]),
        pltpu.make_async_copy(peaks_in, peaks_out, sem.at[1]),
    ]
    for copy in copies:
        copy.start()
    for copy in copies:
        copy.wait()


def kernel(
    R, T, lat_hbm, g1_ref, w1_hbm, g2_ref, w2_hbm, up_hbm, dec_ref, peaks_ref,
    lat, prev, first, second, w1, w2, up, merged, pk_send, pk_recv,
    load_sem, x1_send, x1_recv, rl_send, rl_recv, s_send, s_recv, x3_send, x3_recv, pk_ssem, pk_rsem, known, spread,
):
    r = lax.axis_index("rows")
    t = lax.axis_index("tm")
    n = R * T
    me = r * T + t
    _, frames, cols, C = lat.shape
    half = pk_send.shape[-1]
    SPAN = 2 * REACH + 1

    loads = [
        pltpu.make_async_copy(lat_hbm, lat.at[REACH], load_sem.at[0]),
        pltpu.make_async_copy(w1_hbm, w1.at[:, 0:C, :], load_sem.at[1]),
        pltpu.make_async_copy(w2_hbm, w2.at[:, 0:C, :], load_sem.at[2]),
        pltpu.make_async_copy(up_hbm, up, load_sem.at[3]),
    ]
    for copy in loads:
        copy.start()

    barrier = pltpu.get_barrier_semaphore()

    def there(d):
        return jnp.logical_and(r + d >= 0, r + d < R)

    near = [(d, e) for d in range(-REACH, REACH + 1) for e in range(T) if (d, e) != (0, 0)]

    def greet(d, e):
        pl.semaphore_signal(
            barrier, inc=1, device_id={"rows": r + d, "tm": lax.rem(t + e, T)}, device_id_type=MESH
        )

    second[frames:, :, :] = jnp.zeros_like(second[frames:, :, :])

    @pl.when(t == 0)
    def _():
        second[0:frames, :, :] = jnp.zeros_like(second[0:frames, :, :])

    @pl.when(r == 0)
    def _():
        merged[0] = jnp.zeros_like(merged[0])

    @pl.when(r == R - 1)
    def _():
        merged[2] = jnp.zeros_like(merged[2])

    for d, e in near:
        pl.when(there(d))(functools.partial(greet, d, e))

    first[...] = jnp.zeros_like(first)
    pad = w1.shape[1] - C
    w1[:, C:, :] = jnp.zeros((w1.shape[0], pad, C), BF16)
    w2[:, C:, :] = jnp.zeros((w2.shape[0], pad, C), BF16)
    pk_send[...] = jnp.zeros_like(pk_send)

    width = frames * cols
    q = lax.broadcasted_iota(jnp.int32, (2 * width, 2 * width), 0)
    o = lax.broadcasted_iota(jnp.int32, (2 * width, 2 * width), 1)
    frame = lax.rem(lax.div(q, cols), frames)
    target = frame * (2 * cols) + 2 * lax.rem(q, cols) + lax.div(q, width)
    spread[...] = jnp.where(o == target, 1.0, 0.0).astype(BF16)

    loads[0].wait()
    rows_near = 1 + jnp.minimum(r, REACH) + jnp.minimum(R - 1 - r, REACH)
    pl.semaphore_wait(barrier, rows_near * T - 1)

    offsets = [1, -1, 2, -2]

    def row_copy(d):
        slot = REACH - d
        return pltpu.make_async_remote_copy(
            src_ref=lat.at[REACH], dst_ref=lat.at[slot], send_sem=x1_send.at[slot],
            recv_sem=x1_recv.at[slot], device_id={"rows": r + d}, device_id_type=MESH,
        )

    for d in offsets:
        pl.when(there(d))(lambda d=d: row_copy(d).start())

    stages = [REACH << i for i in range(R.bit_length()) if (REACH << i) < R - 1]

    def tell(i):
        for side, d in enumerate((stages[i], -stages[i])):
            pl.when(there(d))(
                lambda side=side, d=d: pl.semaphore_signal(
                    known.at[i, side], inc=1, device_id={"rows": r + d}, device_id_type=MESH
                )
            )

    def hear(i):
        for side, d in enumerate((stages[i], -stages[i])):
            pl.when(there(-d))(lambda side=side: pl.semaphore_wait(known.at[i, side], 1))

    if stages:
        tell(0)

    def relay(slot):
        return pltpu.make_async_remote_copy(
            src_ref=lat.at[slot], dst_ref=prev.at[slot], send_sem=rl_send.at[slot],
            recv_sem=rl_recv.at[slot], device_id={"tm": t + 1}, device_id_type=MESH,
        )

    gives = t < T - 1
    takes = t > 0
    pl.when(gives)(lambda: relay(REACH).start())

    gain1 = g1_ref[...].astype(F32).reshape(1, C)
    gain2 = g2_ref[...].astype(F32).reshape(1, C)

    def put_first(source, slot, at):
        rows = slice(slot * cols, (slot + 1) * cols)
        values = normed_silu(source[slot].astype(F32).reshape(frames * cols, C), gain1)
        first[at : at + frames, rows, 0:C] = values.reshape(frames, cols, C)
        return values

    def put_peak(i, row):
        pk_send[2 * i : 2 * i + 1, :] = row[:, 0:half]
        pk_send[2 * i + 1 : 2 * i + 2, 0 : C - half] = row[:, half:C]

    put_peak(0, peak_of(put_first(lat, REACH, frames)))

    for d in offsets:
        slot = REACH + d

        @pl.when(there(d))
        def _(d=d, slot=slot):
            row_copy(-d).wait_recv()
            pl.when(gives)(lambda: relay(slot).start())
            put_first(lat, slot, frames)

    for i in range(1, len(stages)):
        hear(i - 1)
        tell(i)

    loads[1].wait()
    parts = taps_part(first, w1, (2,), frames, 3, cols)

    @pl.when(takes)
    def _():
        for d in [0] + offsets:
            slot = REACH + d

            @pl.when(there(d))
            def _(slot=slot):
                relay(slot).wait_recv()
                put_first(prev, slot, 0)

    more = taps_part(first, w1, (0, 1), frames, 3, cols)
    hidden = shifted_sum(parts, more, cols).astype(BF16).astype(F32)
    activated = normed_silu(hidden, gain2).reshape(frames, 3, cols, C)
    zeros = jnp.zeros((frames, cols, C), BF16)
    for j in range(3):
        values = activated[:, j]
        if j != 1:
            values = jnp.where(there(j - 1), values, zeros)
        second[frames:, j * cols : (j + 1) * cols, 0:C] = values

    def hand_on():
        return pltpu.make_async_remote_copy(
            src_ref=second.at[pl.ds(frames, frames)], dst_ref=second.at[pl.ds(0, frames)],
            send_sem=s_send, recv_sem=s_recv, device_id={"tm": t + 1}, device_id_type=MESH,
        )

    pl.when(gives)(lambda: hand_on().start())
    put_peak(1, peak_of(activated[:, 1].reshape(frames * cols, C)))
    loads[2].wait()
    parts = taps_part(second, w2, (2,), frames, 1, cols)
    pl.when(takes)(lambda: hand_on().wait_recv())

    more = taps_part(second, w2, (0, 1), frames, 1, cols)
    block = lat[REACH].astype(F32).reshape(frames * cols, C) + shifted_sum(parts, more, cols)
    block = block.astype(BF16)
    merged[1] = block.reshape(frames, cols, C)
    put_peak(2, peak_of(block))

    def edge_copy(d):
        slot = 1 - d
        return pltpu.make_async_remote_copy(
            src_ref=merged.at[1], dst_ref=merged.at[slot], send_sem=x3_send.at[slot],
            recv_sem=x3_recv.at[slot], device_id={"rows": r + d}, device_id_type=MESH,
        )

    for d in (1, -1):
        pl.when(there(d))(lambda d=d: edge_copy(d).start())

    if stages:
        hear(len(stages) - 1)

    def peak_copy(k):
        peer = lax.rem(me + k, n)
        return pltpu.make_async_remote_copy(
            src_ref=pk_send, dst_ref=pk_recv.at[k], send_sem=pk_ssem.at[k], recv_sem=pk_rsem.at[k],
            device_id={"rows": peer // T, "tm": lax.rem(peer, T)}, device_id_type=MESH,
        )

    def send_peak(k, carry):
        peak_copy(k).start()
        return carry

    lax.fori_loop(1, n, send_peak, 0, unroll=n <= 16)

    loads[3].wait()
    C2 = dec_ref.shape[2]
    own = dot_nt(up[...], block).reshape(3, 3, C2, width)
    upper = own[1] + own[2]
    lower = own[0] + own[1]
    for d in (1, -1):
        pl.when(there(d))(lambda d=d: edge_copy(-d).wait_recv())
    upper = upper + dot_nt(up[0 : 3 * C2], merged[0].reshape(width, C)).reshape(3, C2, width)
    lower = lower + dot_nt(up[6 * C2 :], merged[2].reshape(width, C)).reshape(3, C2, width)
    lane = lax.rem(lax.broadcasted_iota(jnp.int32, (C2, width), 1), cols)

    def columns(sums):
        from_left = jnp.where(lane == 0, 0.0, pltpu.roll(sums[0], 1, 1))
        from_right = jnp.where(lane == cols - 1, 0.0, pltpu.roll(sums[2], width - 1, 1))
        even = from_left + sums[1] + sums[2]
        odd = sums[0] + sums[1] + from_right
        return jnp.concatenate([even, odd], axis=1).astype(BF16)

    narrow = jnp.concatenate([columns(upper), columns(lower)], axis=0)
    wide = dot(narrow, spread[...]).astype(BF16)
    for f in range(frames):
        for j in range(2):
            dec_ref[f, j] = wide[j * C2 : (j + 1) * C2, f * 2 * cols : (f + 1) * 2 * cols]

    def take_peak(k, best):
        peak_copy(k).wait_recv()
        return jnp.maximum(best, pk_recv[k])

    best = lax.fori_loop(1, n, take_peak, pk_send[...], unroll=n <= 16)
    for i in range(3):
        peaks_ref[i : i + 1, 0:half] = best[2 * i : 2 * i + 1, :]
        peaks_ref[i : i + 1, half:C] = best[2 * i + 1 : 2 * i + 2, 0 : C - half]

    def end_peak(k, carry):
        peak_copy(k).wait_send()
        return carry

    lax.fori_loop(1, n, end_peak, 0, unroll=n <= 16)
    for d in offsets:
        pl.when(there(d))(lambda d=d: row_copy(d).wait_send())
    for d in (1, -1):
        pl.when(there(d))(lambda d=d: edge_copy(d).wait_send())

    @pl.when(gives)
    def _():
        for d in [0] + offsets:
            pl.when(there(d))(lambda d=d: relay(REACH + d).wait_send())
        hand_on().wait_send()


def per_device(latent, gain_first, conv_first, gain_second, conv_second, conv_up):
    frames, rows, cols, C = latent.shape
    R, T = lax.axis_size("rows"), lax.axis_size("tm")
    C2 = conv_up.shape[2]
    n = R * T
    if rows != 1 or frames != 2:
        raise ValueError("unsupported block")
    half = 128
    depth = -(-C // 256) * 256
    taps = 27
    vmem = pl.BlockSpec(memory_space=pltpu.VMEM)
    hbm = pl.BlockSpec(memory_space=pl.ANY)
    dma = pltpu.SemaphoreType.DMA
    decoded, peaks = pl.pallas_call(
        functools.partial(kernel, R, T),
        out_shape=(
            jax.ShapeDtypeStruct((frames, 2 * rows, C2, 2 * cols), BF16),
            jax.ShapeDtypeStruct((3, C), F32),
        ),
        in_specs=[hbm, vmem, hbm, vmem, hbm, hbm],
        out_specs=(vmem, vmem),
        scratch_shapes=[
            pltpu.VMEM((2 * REACH + 1, frames, cols, C), BF16),
            pltpu.VMEM((2 * REACH + 1, frames, cols, C), BF16),
            pltpu.VMEM((2 * frames, (2 * REACH + 1) * cols, depth), BF16),
            pltpu.VMEM((2 * frames, 3 * cols, depth), BF16),
            pltpu.VMEM((taps, depth, C), BF16),
            pltpu.VMEM((taps, depth, C), BF16),
            pltpu.VMEM((9 * C2, C), BF16),
            pltpu.VMEM((3, frames, cols, C), BF16),
            pltpu.VMEM((8, half), F32),
            pltpu.VMEM((n, 8, half), F32),
            dma((4,)),
            dma((2 * REACH + 1,)),
            dma((2 * REACH + 1,)),
            dma((2 * REACH + 1,)),
            dma((2 * REACH + 1,)),
            dma,
            dma,
            dma((3,)),
            dma((3,)),
            dma((n,)),
            dma((n,)),
            pltpu.SemaphoreType.REGULAR((R.bit_length(), 2)),
            pltpu.VMEM((2 * frames * cols, 2 * frames * cols), BF16),
        ],
        compiler_params=pltpu.CompilerParams(collective_id=0, has_side_effects=True, vmem_limit_bytes=54 * 2**20),
    )(
        latent.reshape(frames, cols, C),
        gain_first,
        conv_first.reshape(taps, C, C),
        gain_second,
        conv_second.reshape(taps, C, C),
        conv_up.reshape(9 * C2, C),
    )
    return pl.pallas_call(
        finish,
        out_shape=(
            jax.ShapeDtypeStruct(decoded.shape, BF16),
            jax.ShapeDtypeStruct(peaks.shape, F32),
        ),
        in_specs=[vmem, vmem],
        out_specs=(hbm, hbm),
        scratch_shapes=[dma((2,))],
    )(decoded, peaks)


def solution(mesh):
    return jax.shard_map(
        per_device,
        mesh=mesh,
        in_specs=(P(("clip", "tm"), "rows", None, None), P(), P(), P(), P(), P()),
        out_specs=(P(("clip", "tm"), "rows", None, None), P("clip", None)),
        check_vma=False,
    )
```

profile of v0, /device:TPU:0, one launch (start us, length us, event | category | flops | bytes accessed | tf_op | source)
XLA Modules:
  0.0 23.1 jit_solution(2479263718844163633)
XLA Ops:
  0.6 21.0 %shard_map.77 = (bf16[2,2,96,128]{3,2,1,0:T(8,128)(2,1)}, f32[3,192]{1,0:T(4,128)}) custom-call(bf16[2,64,192]{2,1,0:T(8,128)(2,1)} %bitcast.7, bf16[192]{0:T(256)(128)(2,1)} %g1_ref.1, bf16[27,192,192]{2,1,0:T(8,128)(2,1)} %bitcast.4, bf16[192]{0:T(256)(128)(2,1)} %g2_ref.1, bf16[27,192,192]{2,1,0:T(8,128)(2,1)} %bitcast.5, bf16[864,192]{1,0:T(8,128)(2,1)} %bitcast.6), custom_call_target="tpu_custom_call" | custom-call | tf_op jit(solution)/shard_map/pallas_call | solution.py:336
  21.6 1.6 %shard_map.78 = (bf16[2,2,96,128]{3,2,1,0:T(8,128)(2,1)}, f32[3,192]{1,0:T(4,128)}) custom-call(bf16[2,2,96,128]{3,2,1,0:T(8,128)(2,1)} %get-tuple-element.4.dec_in, f32[3,192]{1,0:T(4,128)} %get-tuple-element.5.peaks_in), custom_call_target="tpu_custom_call" | custom-call | tf_op jit(solution)/shard_map/pallas_call | solution.py:378
where the time goes:
time: 23.3 us; the launch traced here: 23.1 us
  Pallas kernels  22.5 us (97%)
  between operations  0.64 us (3%)
    pallas_call x1, Pallas kernels, per_device(): pl.pallas_call(functools.partial(kernel, R, T), out_shape=(jax.ShapeDtype...  21 us
    pallas_call x1, Pallas kernels, per_device(): pl.pallas_call(finish, out_shape=(jax.ShapeDtypeStruct(decoded.shape, BF1...  1.55 us

commit v1 on v0

v1 whole, which is shorter than its diff:
```python
import functools

import jax
import jax.numpy as jnp
from jax import lax
from jax.experimental import pallas as pl
from jax.experimental.pallas import tpu as pltpu
from jax.sharding import PartitionSpec as P

MESH = pl.DeviceIdType.MESH
BF16 = jnp.bfloat16
F32 = jnp.float32
REACH = 2
LANES = 128


def normed_silu(values, gain):
    scale = lax.rsqrt(jnp.mean(values * values, axis=-1, keepdims=True) + 1e-06)
    u = values * scale * gain
    return u / (1.0 + jnp.exp(-u))


def peak_of(values):
    return jnp.max(jnp.abs(values), axis=0, keepdims=True)


def dot(a, b):
    return jnp.dot(a, b, preferred_element_type=F32)


def dot_nt(a, b):
    return lax.dot_general(a, b, (((1,), (1,)), ((), ())), preferred_element_type=F32)


def packed(values, cols):
    low = values[:, 0:LANES].reshape(2, cols, LANES)
    high = jnp.concatenate([values[0:cols, LANES:], values[cols:, LANES:]], axis=1)
    return jnp.concatenate([low, high[None]], axis=0).astype(BF16)


def frames_of(buf):
    high = buf[2]
    turned = pltpu.roll(high.astype(F32), LANES // 2, 1).astype(BF16)
    return jnp.concatenate([buf[0], high], axis=1), jnp.concatenate([buf[1], turned], axis=1)


def finish(dec_in, peaks_in, dec_out, peaks_out, sem):
    copies = [
        pltpu.make_async_copy(dec_in, dec_out, sem.at[0]),
        pltpu.make_async_copy(peaks_in, peaks_out, sem.at[1]),
    ]
    for copy in copies:
        copy.start()
    for copy in copies:
        copy.wait()


def kernel(
    R, T, lat_hbm, g1_hbm, w1_hbm, g2_hbm, w2_hbm, up_hbm, dec_ref, peaks_ref,
    lat, g1, g2, rows_in, hist, acc, second, past, w1, w2, up, merged,
    pk1_send, pk1_recv, pk2_send, pk2_recv,
    load_sem, x1_send, x1_recv, rl_send, rl_recv, s_send, s_recv, x3_send, x3_recv,
    pk1_ssem, pk1_rsem, pk2_ssem, pk2_rsem, known, spread,
):
    r = lax.axis_index("rows")
    t = lax.axis_index("tm")
    n = R * T
    me = r * T + t
    frames, cols, C = lat.shape
    width = frames * cols

    def there(d):
        return jnp.logical_and(r + d >= 0, r + d < R)

    barrier = pltpu.get_barrier_semaphore()
    near = [(d, e) for d in range(-REACH, REACH + 1) for e in range(T) if (d, e) != (0, 0)]

    def greet(d, e):
        pl.semaphore_signal(
            barrier, inc=1, device_id={"rows": r + d, "tm": lax.rem(t + e, T)}, device_id_type=MESH
        )

    loads = [
        pltpu.make_async_copy(lat_hbm, lat, load_sem.at[0]),
        pltpu.make_async_copy(g1_hbm, g1, load_sem.at[1]),
        pltpu.make_async_copy(g2_hbm, g2, load_sem.at[2]),
        pltpu.make_async_copy(w1_hbm, w1.at[:, 0:C, :], load_sem.at[3]),
        pltpu.make_async_copy(w2_hbm, w2.at[:, 0:C, :], load_sem.at[4]),
        pltpu.make_async_copy(up_hbm, up, load_sem.at[5]),
    ]
    loads[0].start()
    loads[1].start()
    for d, e in near:
        pl.when(there(d))(functools.partial(greet, d, e))
    for copy in loads[2:]:
        copy.start()

    @pl.when(r == 0)
    def _():
        merged[0] = jnp.zeros_like(merged[0])

    @pl.when(r == R - 1)
    def _():
        merged[2] = jnp.zeros_like(merged[2])

    pad = w1.shape[1] - C
    w1[:, C:, :] = jnp.zeros((w1.shape[0], pad, C), BF16)
    w2[:, C:, :] = jnp.zeros((w2.shape[0], pad, C), BF16)
    pk1_send[...] = jnp.zeros_like(pk1_send)
    pk2_send[...] = jnp.zeros_like(pk2_send)

    q = lax.broadcasted_iota(jnp.int32, (2 * width, 2 * width), 0)
    o = lax.broadcasted_iota(jnp.int32, (2 * width, 2 * width), 1)
    frame = lax.rem(lax.div(q, cols), frames)
    target = frame * (2 * cols) + 2 * lax.rem(q, cols) + lax.div(q, width)
    spread[...] = jnp.where(o == target, 1.0, 0.0).astype(BF16)

    loads[0].wait()
    loads[1].wait()
    gain1 = g1[...].astype(F32).reshape(1, C)
    own_first = normed_silu(lat[...].astype(F32).reshape(width, C), gain1)
    rows_in[REACH] = packed(own_first, cols)

    rows_near = 1 + jnp.minimum(r, REACH) + jnp.minimum(R - 1 - r, REACH)
    pl.semaphore_wait(barrier, rows_near * T - 1)

    side = 1 - 2 * lax.rem(r, 2)

    def row_copy(d):
        slot = REACH - d
        return pltpu.make_async_remote_copy(
            src_ref=rows_in.at[REACH], dst_ref=rows_in.at[slot], send_sem=x1_send.at[slot],
            recv_sem=x1_recv.at[slot], device_id={"rows": r + d}, device_id_type=MESH,
        )

    for d in (-side, side, 2 * side, -2 * side):
        pl.when(there(d))(lambda d=d: row_copy(d).start())

    def relay(slot):
        return pltpu.make_async_remote_copy(
            src_ref=rows_in.at[slot], dst_ref=hist.at[slot], send_sem=rl_send.at[slot],
            recv_sem=rl_recv.at[slot], device_id={"tm": t + 1}, device_id_type=MESH,
        )

    gives = t < T - 1
    takes = t > 0
    pl.when(gives)(lambda: relay(REACH).start())

    stages = [REACH << i for i in range(R.bit_length()) if (REACH << i) < R - 1]

    def tell(i):
        for way, d in enumerate((stages[i], -stages[i])):
            pl.when(there(d))(
                lambda way=way, d=d: pl.semaphore_signal(
                    known.at[i, way], inc=1, device_id={"rows": r + d}, device_id_type=MESH
                )
            )

    def hear(i):
        for way, d in enumerate((stages[i], -stages[i])):
            pl.when(there(-d))(lambda way=way: pl.semaphore_wait(known.at[i, way], 1))

    if stages:
        tell(0)

    def put_peak(ref, i, row):
        ref[2 * i : 2 * i + 1, :] = row[:, 0:LANES]
        ref[2 * i + 1 : 2 * i + 2, 0 : C - LANES] = row[:, LANES:C]

    put_peak(pk1_send, 0, peak_of(own_first.astype(BF16).astype(F32)))

    def contribute(buf, pairs, past_frames, fresh=False):
        f0, f1 = frames_of(buf)
        both = jnp.concatenate([f0, f1], axis=0)
        tap = 0 if past_frames else 2
        for at, j in pairs:
            for k in range(3):
                main = dot(both, w1[(tap * 3 + j) * 3 + k])
                extra = dot(f1 if past_frames else f0, w1[(3 + j) * 3 + k])
                early, late = main[0:cols], main[cols:]
                if past_frames:
                    early = early + extra
                else:
                    late = late + extra
                if fresh:
                    acc[k, at, 0:cols] = early
                    acc[k, at, cols:] = late
                else:
                    acc[k, at, 0:cols] += early
                    acc[k, at, cols:] += late

    own_pairs = [(0, 2), (1, 1), (2, 0)]

    def pairs_of(s, far):
        return [(1 + s, 1 + s)] if far else [(1, 1 + s), (1 + s, 1)]

    loads[3].wait()
    contribute(rows_in.at[REACH], own_pairs, False, fresh=True)

    @pl.when(takes)
    def _():
        relay(REACH).wait_recv()
        contribute(hist.at[REACH], own_pairs, True)

    steps = [(side, False), (side, True), (-side, True), (-side, False)]

    def fresh_row(s, far):
        d = 2 * s if far else s
        slot = REACH + d

        @pl.when(there(d))
        def _():
            row_copy(-d).wait_recv()
            pl.when(gives)(lambda: relay(slot).start())
            contribute(rows_in.at[slot], pairs_of(s, far), False)

    def past_row(s, far):
        d = 2 * s if far else s
        slot = REACH + d

        @pl.when(jnp.logical_and(takes, there(d)))
        def _():
            relay(slot).wait_recv()
            contribute(hist.at[slot], pairs_of(s, far), True)

    fresh_row(*steps[0])
    fresh_row(*steps[1])
    past_row(*steps[0])
    fresh_row(*steps[2])
    past_row(*steps[1])
    fresh_row(*steps[3])
    past_row(*steps[2])
    past_row(*steps[3])

    for i in range(1, len(stages)):
        hear(i - 1)
        tell(i)

    lane0 = lax.rem(lax.broadcasted_iota(jnp.int32, (width, 1), 0), cols)

    def shifted_sum(left, middle, right):
        left = jnp.where(lane0 == 0, 0.0, pltpu.roll(left, 1, 0))
        right = jnp.where(lane0 == cols - 1, 0.0, pltpu.roll(right, width - 1, 0))
        return left + middle + right

    loads[2].wait()
    gain2 = g2[...].astype(F32).reshape(1, C)
    for at in range(3):
        hidden = shifted_sum(acc[0, at], acc[1, at], acc[2, at]).astype(BF16).astype(F32)
        values = normed_silu(hidden, gain2)
        if at != 1:
            values = jnp.where(there(at - 1), values, 0.0)
        else:
            put_peak(pk1_send, 1, peak_of(values.astype(BF16).astype(F32)))
        second[at] = packed(values, cols)

    def hand_on():
        return pltpu.make_async_remote_copy(
            src_ref=second, dst_ref=past,
            send_sem=s_send, recv_sem=s_recv, device_id={"tm": t + 1}, device_id_type=MESH,
        )

    pl.when(gives)(lambda: hand_on().start())

    if stages:
        hear(len(stages) - 1)

    def peer_of(i):
        p = jnp.where(2 * r >= R, i, n - 2 - i)
        return jnp.where(p >= me, p + 1, p)

    def peak_copy(src, dst, ssem, rsem, peer, owner):
        return pltpu.make_async_remote_copy(
            src_ref=src, dst_ref=dst.at[owner], send_sem=ssem.at[peer], recv_sem=rsem.at[owner],
            device_id={"rows": peer // T, "tm": lax.rem(peer, T)}, device_id_type=MESH,
        )

    def send_peaks(src, dst, ssem, rsem):
        def step(i, carry):
            peak_copy(src, dst, ssem, rsem, peer_of(i), me).start()
            return carry

        lax.fori_loop(0, n - 1, step, 0, unroll=n <= 16)

    def take_peaks(src, dst, ssem, rsem):
        def step(i, best):
            peer = peer_of(n - 2 - i)
            peak_copy(src, dst, ssem, rsem, peer, peer).wait_recv()
            return jnp.maximum(best, dst[peer])

        return lax.fori_loop(0, n - 1, step, src[...], unroll=n <= 16)

    def end_peaks(src, dst, ssem, rsem):
        def step(i, carry):
            peak_copy(src, dst, ssem, rsem, peer_of(i), me).wait_send()
            return carry

        lax.fori_loop(0, n - 1, step, 0, unroll=n <= 16)

    early = (pk1_send, pk1_recv, pk1_ssem, pk1_rsem)
    last = (pk2_send, pk2_recv, pk2_ssem, pk2_rsem)
    send_peaks(*early)

    loads[4].wait()

    def second_part(buf, past_frames):
        pieces = [frames_of(buf.at[j]) for j in range(3)]
        f0 = jnp.concatenate([piece[0] for piece in pieces], axis=1)
        f1 = jnp.concatenate([piece[1] for piece in pieces], axis=1)
        both = jnp.concatenate([f0, f1], axis=0)
        tap = 0 if past_frames else 2
        for k in range(3):
            main = dot(both, jnp.concatenate([w2[(tap * 3 + j) * 3 + k] for j in range(3)], axis=0))
            extra = dot(
                f1 if past_frames else f0,
                jnp.concatenate([w2[(3 + j) * 3 + k] for j in range(3)], axis=0),
            )
            early, late = main[0:cols], main[cols:]
            if past_frames:
                acc[k, 0, 0:cols] += early + extra
                acc[k, 0, cols:] += late
            else:
                acc[k, 0, 0:cols] = early
                acc[k, 0, cols:] = late + extra

    second_part(second, False)

    @pl.when(takes)
    def _():
        hand_on().wait_recv()
        second_part(past, True)

    block = lat[...].astype(F32).reshape(width, C) + shifted_sum(acc[0, 0], acc[1, 0], acc[2, 0])
    block = block.astype(BF16)
    wide_block = block.astype(F32)
    merged[1] = packed(wide_block, cols)
    put_peak(pk2_send, 0, peak_of(wide_block))
    send_peaks(*last)

    def edge_copy(d):
        slot = 1 - d
        return pltpu.make_async_remote_copy(
            src_ref=merged.at[1], dst_ref=merged.at[slot], send_sem=x3_send.at[slot],
            recv_sem=x3_recv.at[slot], device_id={"rows": r + d}, device_id_type=MESH,
        )

    for d in (-side, side):
        pl.when(there(d))(lambda d=d: edge_copy(d).start())

    loads[5].wait()
    C2 = dec_ref.shape[2]
    own = dot_nt(up[...], block).reshape(3, 3, C2, width)
    upper = own[1] + own[2]
    lower = own[0] + own[1]

    def edge_row(slot):
        f0, f1 = frames_of(merged.at[slot])
        return jnp.concatenate([f0, f1], axis=0)[:, 0:C]

    for d in (side, -side):
        pl.when(there(d))(lambda d=d: edge_copy(-d).wait_recv())
    upper = upper + dot_nt(up[0 : 3 * C2], edge_row(0)).reshape(3, C2, width)
    lower = lower + dot_nt(up[6 * C2 :], edge_row(2)).reshape(3, C2, width)
    lane = lax.rem(lax.broadcasted_iota(jnp.int32, (C2, width), 1), cols)

    def columns(sums):
        from_left = jnp.where(lane == 0, 0.0, pltpu.roll(sums[0], 1, 1))
        from_right = jnp.where(lane == cols - 1, 0.0, pltpu.roll(sums[2], width - 1, 1))
        even = from_left + sums[1] + sums[2]
        odd = sums[0] + sums[1] + from_right
        return jnp.concatenate([even, odd], axis=1).astype(BF16)

    narrow = jnp.concatenate([columns(upper), columns(lower)], axis=0)
    wide = dot(narrow, spread[...]).astype(BF16)
    for f in range(frames):
        for j in range(2):
            dec_ref[f, j] = wide[j * C2 : (j + 1) * C2, f * 2 * cols : (f + 1) * 2 * cols]

    best = take_peaks(*early)
    for i in range(2):
        peaks_ref[i : i + 1, 0:LANES] = best[2 * i : 2 * i + 1, :]
        peaks_ref[i : i + 1, LANES:C] = best[2 * i + 1 : 2 * i + 2, 0 : C - LANES]
    best = take_peaks(*last)
    peaks_ref[2:3, 0:LANES] = best[0:1, :]
    peaks_ref[2:3, LANES:C] = best[1:2, 0 : C - LANES]

    end_peaks(*early)
    end_peaks(*last)
    for d in (1, -1, 2, -2):
        pl.when(there(d))(lambda d=d: row_copy(d).wait_send())
    for d in (1, -1):
        pl.when(there(d))(lambda d=d: edge_copy(d).wait_send())

    @pl.when(gives)
    def _():
        for d in (0, 1, -1, 2, -2):
            pl.when(there(d))(lambda d=d: relay(REACH + d).wait_send())
        hand_on().wait_send()


def per_device(latent, gain_first, conv_first, gain_second, conv_second, conv_up):
    frames, rows, cols, C = latent.shape
    R, T = lax.axis_size("rows"), lax.axis_size("tm")
    C2 = conv_up.shape[2]
    n = R * T
    if rows != 1 or frames != 2 or 2 * C != 3 * LANES:
        raise ValueError("unsupported block")
    depth = 2 * LANES
    taps = conv_first.shape[0] * conv_first.shape[1] * conv_first.shape[2]
    vmem = pl.BlockSpec(memory_space=pltpu.VMEM)
    hbm = pl.BlockSpec(memory_space=pltpu.HBM)
    dma = pltpu.SemaphoreType.DMA
    span = 2 * REACH + 1
    width = frames * cols
    decoded, peaks = pl.pallas_call(
        functools.partial(kernel, R, T),
        out_shape=(
            pltpu.VMEM((frames, 2 * rows, C2, 2 * cols), BF16),
            pltpu.VMEM((3, C), F32),
        ),
        in_specs=[hbm] * 6,
        out_specs=(vmem, vmem),
        scratch_shapes=[
            pltpu.VMEM((frames, cols, C), BF16),
            pltpu.VMEM((C,), BF16),
            pltpu.VMEM((C,), BF16),
            pltpu.VMEM((span, 3, cols, LANES), BF16),
            pltpu.VMEM((span, 3, cols, LANES), BF16),
            pltpu.VMEM((3, 3, width, C), F32),
            pltpu.VMEM((3, 3, cols, LANES), BF16),
            pltpu.VMEM((3, 3, cols, LANES), BF16),
            pltpu.VMEM((taps, depth, C), BF16),
            pltpu.VMEM((taps, depth, C), BF16),
            pltpu.VMEM((9 * C2, C), BF16),
            pltpu.VMEM((3, 3, cols, LANES), BF16),
            pltpu.VMEM((4, LANES), F32),
            pltpu.VMEM((n, 4, LANES), F32),
            pltpu.VMEM((2, LANES), F32),
            pltpu.VMEM((n, 2, LANES), F32),
            dma((6,)),
            dma((span,)),
            dma((span,)),
            dma((span,)),
            dma((span,)),
            dma,
            dma,
            dma((3,)),
            dma((3,)),
            dma((n,)),
            dma((n,)),
            dma((n,)),
            dma((n,)),
            pltpu.SemaphoreType.REGULAR((R.bit_length(), 2)),
            pltpu.VMEM((2 * width, 2 * width), BF16),
        ],
        compiler_params=pltpu.CompilerParams(collective_id=0, has_side_effects=True, vmem_limit_bytes=54 * 2**20),
    )(
        latent.reshape(frames, cols, C),
        gain_first,
        conv_first.reshape(taps, C, C),
        gain_second,
        conv_second.reshape(taps, C, C),
        conv_up.reshape(9 * C2, C),
    )
    return pl.pallas_call(
        finish,
        out_shape=(
            jax.ShapeDtypeStruct(decoded.shape, BF16),
            jax.ShapeDtypeStruct(peaks.shape, F32),
        ),
        in_specs=[vmem, vmem],
        out_specs=(hbm, hbm),
        scratch_shapes=[dma((2,))],
        compiler_params=pltpu.CompilerParams(vmem_limit_bytes=2**20),
    )(decoded, peaks)


def solution(mesh):
    return jax.shard_map(
        per_device,
        mesh=mesh,
        in_specs=(P(("clip", "tm"), "rows", None, None), P(), P(), P(), P(), P()),
        out_specs=(P(("clip", "tm"), "rows", None, None), P("clip", None)),
        check_vma=False,
    )
```

time: 23.3 us -> 19 us (0.82)
  Pallas kernels: 22.5 us -> 18.2 us
    pallas_call x1, Pallas kernels: 21 us -> 17.6 us  [per_device(): pl.pallas_call(functools.partial(kernel, R, T), out_shape=(pltpu.VMEM((fr...]
    pallas_call x1, Pallas kernels: 1.55 us -> 0.66 us  [per_device(): pl.pallas_call(finish, out_shape=(jax.ShapeDtypeStruct(decoded.shape, BF1...]
where the time goes in v1:
time: 19 us; the launch traced here: 18.9 us
  Pallas kernels  18.2 us (96%)
  between operations  0.64 us (3%)
    pallas_call x1, Pallas kernels, per_device(): pl.pallas_call(functools.partial(kernel, R, T), out_shape=(pltpu.VMEM((fr...  17.6 us
    pallas_call x1, Pallas kernels, per_device(): pl.pallas_call(finish, out_shape=(jax.ShapeDtypeStruct(decoded.shape, BF1...  0.66 us

profile of v1, /device:TPU:0, one launch (start us, length us, event | category | flops | bytes accessed | tf_op | source)
XLA Modules:
  0.0 18.9 jit_solution(10949012373127050069)
XLA Ops:
  0.6 17.6 %shard_map.77 = (bf16[2,2,96,128]{3,2,1,0:T(8,128)(2,1)S(1)}, f32[3,192]{1,0:T(4,128)S(1)}) custom-call(bf16[2,64,192]{2,1,0:T(8,128)(2,1)} %bitcast.7, bf16[192]{0:T(256)(128)(2,1)} %g1_hbm.1, bf16[27,192,192]{2,1,0:T(8,128)(2,1)} %bitcast.4, bf16[192]{0:T(256)(128)(2,1)} %g2_hbm.1, bf16[27,192,192]{2,1,0:T(8,128)(2,1)} %bitcast.5, bf16[864,192]{1,0:T(8,128)(2,1)} %bitcast.6), custom_call_target="tpu_custom_call" | custom-call | tf_op jit(solution)/shard_map/pallas_call | solution.py:415
  18.2 0.7 %shard_map.78 = (bf16[2,2,96,128]{3,2,1,0:T(8,128)(2,1)}, f32[3,192]{1,0:T(4,128)}) custom-call(bf16[2,2,96,128]{3,2,1,0:T(8,128)(2,1)S(1)} %get-tuple-element.4.dec_in, f32[3,192]{1,0:T(4,128)S(1)} %get-tuple-element.5.peaks_in), custom_call_target="tpu_custom_call" | custom-call | tf_op jit(solution)/shard_map/pallas_call | solution.py:465

commit v2 on v1

--- a/solution.py
+++ b/solution.py
@@ -57,8 +57,8 @@
 
 def kernel(
     R, T, lat_hbm, g1_hbm, w1_hbm, g2_hbm, w2_hbm, up_hbm, dec_ref, peaks_ref,
-    lat, g1, g2, rows_in, hist, acc, second, past, w1, w2, up, merged,
-    pk1_send, pk1_recv, pk2_send, pk2_recv,
+    lat, g1, g2, rows_in, hist, acc, mix, second, past, w1, w2, up, merged,
+    pk1_send, pk1_recv, pk2_send, pk2_recv, pk_second,
     load_sem, x1_send, x1_recv, rl_send, rl_recv, s_send, s_recv, x3_send, x3_recv,
     pk1_ssem, pk1_rsem, pk2_ssem, pk2_rsem, known, spread,
 ):
@@ -92,8 +92,8 @@
     loads[1].start()
     for d, e in near:
         pl.when(there(d))(functools.partial(greet, d, e))
-    for copy in loads[2:]:
-        copy.start()
+    loads[3].start()
+    loads[2].start()
 
     @pl.when(r == 0)
     def _():
@@ -103,11 +103,18 @@
     def _():
         merged[2] = jnp.zeros_like(merged[2])
 
+    for d in (-2, -1, 1, 2):
+
+        @pl.when(jnp.logical_not(there(d)))
+        def _(d=d):
+            rows_in[REACH + d] = jnp.zeros_like(rows_in[REACH + d])
+            hist[REACH + d] = jnp.zeros_like(hist[REACH + d])
+            if abs(d) == 1:
+                second[1 + d] = jnp.zeros_like(second[1 + d])
+
     pad = w1.shape[1] - C
     w1[:, C:, :] = jnp.zeros((w1.shape[0], pad, C), BF16)
     w2[:, C:, :] = jnp.zeros((w2.shape[0], pad, C), BF16)
-    pk1_send[...] = jnp.zeros_like(pk1_send)
-    pk2_send[...] = jnp.zeros_like(pk2_send)
 
     q = lax.broadcasted_iota(jnp.int32, (2 * width, 2 * width), 0)
     o = lax.broadcasted_iota(jnp.int32, (2 * width, 2 * width), 1)
@@ -163,78 +170,59 @@
     if stages:
         tell(0)
 
-    def put_peak(ref, i, row):
-        ref[2 * i : 2 * i + 1, :] = row[:, 0:LANES]
-        ref[2 * i + 1 : 2 * i + 2, 0 : C - LANES] = row[:, LANES:C]
-
-    put_peak(pk1_send, 0, peak_of(own_first.astype(BF16).astype(F32)))
-
-    def contribute(buf, pairs, past_frames, fresh=False):
-        f0, f1 = frames_of(buf)
+    def two_rows(row):
+        rest = jnp.concatenate([row[:, LANES:C], jnp.zeros((1, 2 * LANES - C), F32)], axis=1)
+        return jnp.concatenate([row[:, 0:LANES], rest], axis=0)
+
+    pk1_send[...] = two_rows(peak_of(own_first.astype(BF16).astype(F32))).astype(BF16)
+
+    def contribute(source, past_frames):
+        f0, f1 = frames_of(source.at[REACH])
         both = jnp.concatenate([f0, f1], axis=0)
         tap = 0 if past_frames else 2
-        for at, j in pairs:
+        for at in range(3):
+            j = 2 - at
             for k in range(3):
                 main = dot(both, w1[(tap * 3 + j) * 3 + k])
                 extra = dot(f1 if past_frames else f0, w1[(3 + j) * 3 + k])
                 early, late = main[0:cols], main[cols:]
                 if past_frames:
-                    early = early + extra
+                    acc[k, at, 0:cols] += early + extra
+                    acc[k, at, cols:] += late
                 else:
-                    late = late + extra
-                if fresh:
                     acc[k, at, 0:cols] = early
-                    acc[k, at, cols:] = late
-                else:
-                    acc[k, at, 0:cols] += early
-                    acc[k, at, cols:] += late
-
-    own_pairs = [(0, 2), (1, 1), (2, 0)]
-
-    def pairs_of(s, far):
-        return [(1 + s, 1 + s)] if far else [(1, 1 + s), (1 + s, 1)]
+                    acc[k, at, cols:] = late + extra
+
+    def contribute_side(source, s, past_frames):
+        n0, n1 = frames_of(source.at[REACH + s])
+        f0, f1 = frames_of(source.at[REACH + 2 * s])
+        near_rows = jnp.concatenate([n0, n1], axis=0)
+        all_rows = jnp.concatenate([n0, n1, f0, f1], axis=0)
+        near_one, far_one = (n1, f1) if past_frames else (n0, f0)
+        ones = jnp.concatenate([near_one, far_one], axis=0)
+        tap = 0 if past_frames else 2
+        mixed = slice(0, cols) if past_frames else slice(cols, width)
+        for k in range(3):
+            main = dot(all_rows, w1[(tap * 3 + 1 + s) * 3 + k])
+            extra = dot(ones, w1[(3 + 1 + s) * 3 + k])
+            acc[k, 1] += main[0:width]
+            acc[k, 1, mixed] += extra[0:cols]
+            acc[k, 1 + s] += main[width:] + dot(near_rows, w1[(tap * 3 + 1) * 3 + k])
+            acc[k, 1 + s, mixed] += extra[cols:] + dot(near_one, w1[(3 + 1) * 3 + k])
 
     loads[3].wait()
-    contribute(rows_in.at[REACH], own_pairs, False, fresh=True)
-
-    @pl.when(takes)
-    def _():
-        relay(REACH).wait_recv()
-        contribute(hist.at[REACH], own_pairs, True)
-
-    steps = [(side, False), (side, True), (-side, True), (-side, False)]
-
-    def fresh_row(s, far):
-        d = 2 * s if far else s
-        slot = REACH + d
-
+    loads[4].start()
+    loads[5].start()
+    contribute(rows_in, False)
+
+    def await_row(d):
         @pl.when(there(d))
         def _():
             row_copy(-d).wait_recv()
-            pl.when(gives)(lambda: relay(slot).start())
-            contribute(rows_in.at[slot], pairs_of(s, far), False)
-
-    def past_row(s, far):
-        d = 2 * s if far else s
-        slot = REACH + d
-
-        @pl.when(jnp.logical_and(takes, there(d)))
-        def _():
-            relay(slot).wait_recv()
-            contribute(hist.at[slot], pairs_of(s, far), True)
-
-    fresh_row(*steps[0])
-    fresh_row(*steps[1])
-    past_row(*steps[0])
-    fresh_row(*steps[2])
-    past_row(*steps[1])
-    fresh_row(*steps[3])
-    past_row(*steps[2])
-    past_row(*steps[3])
-
-    for i in range(1, len(stages)):
-        hear(i - 1)
-        tell(i)
+            pl.when(gives)(lambda: relay(REACH + d).start())
+
+    def await_past(d):
+        pl.when(there(d))(lambda: relay(REACH + d).wait_recv())
 
     lane0 = lax.rem(lax.broadcasted_iota(jnp.int32, (width, 1), 0), cols)
 
@@ -243,27 +231,72 @@
         right = jnp.where(lane0 == cols - 1, 0.0, pltpu.roll(right, width - 1, 0))
         return left + middle + right
 
+    def activate(o):
+        if isinstance(o, int):
+            activate_row(o)
+        else:
+            pl.when(there(o))(lambda: activate_row(o))
+
+    def activate_row(o):
+        at = 1 + o
+        hidden = shifted_sum(acc[0, at], acc[1, at], acc[2, at]).astype(BF16).astype(F32)
+        values = normed_silu(hidden, gain2)
+        if isinstance(o, int):
+            pk_second[...] = two_rows(peak_of(values.astype(BF16).astype(F32)))
+        second[at] = packed(values, cols)
+
+    def hand_on(o):
+        at = 1 + o
+        return pltpu.make_async_remote_copy(
+            src_ref=second.at[at], dst_ref=past.at[at],
+            send_sem=s_send.at[at], recv_sem=s_recv.at[at], device_id={"tm": t + 1}, device_id_type=MESH,
+        )
+
     loads[2].wait()
     gain2 = g2[...].astype(F32).reshape(1, C)
-    for at in range(3):
-        hidden = shifted_sum(acc[0, at], acc[1, at], acc[2, at]).astype(BF16).astype(F32)
-        values = normed_silu(hidden, gain2)
-        if at != 1:
-            values = jnp.where(there(at - 1), values, 0.0)
+
+    def second_conv(offsets, fresh, has_past):
+        rows = [1 + o for o in offsets]
+
+        def frames_at(source):
+            pieces = [frames_of(source.at[j]) for j in rows]
+            return [jnp.concatenate([piece[f] for piece in pieces], axis=1) for f in range(2)]
+
+        def taps_at(i, k):
+            return [w2[(i * 3 + j) * 3 + k] for j in rows]
+
+        def add(k, part, value):
+            if fresh:
+                mix[k, part] = value
+            else:
+                mix[k, part] += value
+
+        f0, f1 = frames_at(second)
+        if has_past:
+            for o in offsets:
+                hand_on(o).wait_recv()
+            h0, h1 = frames_at(past)
+            early = jnp.concatenate([h0, h1, f0], axis=1)
+            late = jnp.concatenate([h1, f0, f1], axis=1)
+            lhs = jnp.concatenate([early, late], axis=0)
+            for k in range(3):
+                taps = [tap for i in range(3) for tap in taps_at(i, k)]
+                add(k, slice(0, width), dot(lhs, jnp.concatenate(taps, axis=0)))
         else:
-            put_peak(pk1_send, 1, peak_of(values.astype(BF16).astype(F32)))
-        second[at] = packed(values, cols)
-
-    def hand_on():
-        return pltpu.make_async_remote_copy(
-            src_ref=second, dst_ref=past,
-            send_sem=s_send, recv_sem=s_recv, device_id={"tm": t + 1}, device_id_type=MESH,
-        )
-
-    pl.when(gives)(lambda: hand_on().start())
-
-    if stages:
-        hear(len(stages) - 1)
+            both = jnp.concatenate([f0, f1], axis=0)
+            for k in range(3):
+                main = dot(both, jnp.concatenate(taps_at(2, k), axis=0))
+                extra = dot(f0, jnp.concatenate(taps_at(1, k), axis=0))
+                add(k, slice(0, cols), main[0:cols])
+                add(k, slice(cols, width), main[cols:] + extra)
+
+    def meet():
+        for i in range(1, len(stages)):
+            hear(i - 1)
+            tell(i)
+
+    def pass_on(o):
+        pl.when(gives)(lambda: hand_on(o).start())
 
     def peer_of(i):
         p = jnp.where(2 * r >= R, i, n - 2 - i)
@@ -286,9 +319,9 @@
         def step(i, best):
             peer = peer_of(n - 2 - i)
             peak_copy(src, dst, ssem, rsem, peer, peer).wait_recv()
-            return jnp.maximum(best, dst[peer])
-
-        return lax.fori_loop(0, n - 1, step, src[...], unroll=n <= 16)
+            return jnp.maximum(best, dst[peer].astype(F32))
+
+        return lax.fori_loop(0, n - 1, step, src[...].astype(F32), unroll=n <= 16)
 
     def end_peaks(src, dst, ssem, rsem):
         def step(i, carry):
@@ -299,42 +332,64 @@
 
     early = (pk1_send, pk1_recv, pk1_ssem, pk1_rsem)
     last = (pk2_send, pk2_recv, pk2_ssem, pk2_rsem)
-    send_peaks(*early)
-
-    loads[4].wait()
-
-    def second_part(buf, past_frames):
-        pieces = [frames_of(buf.at[j]) for j in range(3)]
-        f0 = jnp.concatenate([piece[0] for piece in pieces], axis=1)
-        f1 = jnp.concatenate([piece[1] for piece in pieces], axis=1)
-        both = jnp.concatenate([f0, f1], axis=0)
-        tap = 0 if past_frames else 2
-        for k in range(3):
-            main = dot(both, jnp.concatenate([w2[(tap * 3 + j) * 3 + k] for j in range(3)], axis=0))
-            extra = dot(
-                f1 if past_frames else f0,
-                jnp.concatenate([w2[(3 + j) * 3 + k] for j in range(3)], axis=0),
-            )
-            early, late = main[0:cols], main[cols:]
-            if past_frames:
-                acc[k, 0, 0:cols] += early + extra
-                acc[k, 0, cols:] += late
-            else:
-                acc[k, 0, 0:cols] = early
-                acc[k, 0, cols:] = late + extra
-
-    second_part(second, False)
+
+    def first_peaks():
+        if stages:
+            hear(len(stages) - 1)
+        send_peaks(*early)
+
+    def beside(source, s, past_frames):
+        pl.when(there(s))(lambda: contribute_side(source, s, past_frames))
+
+    @pl.when(jnp.logical_not(takes))
+    def _():
+        await_row(-2)
+        meet()
+        await_row(side)
+        await_row(2)
+        beside(rows_in, side, False)
+        activate(side)
+        pass_on(side)
+        await_row(-side)
+        beside(rows_in, -side, False)
+        activate(0)
+        pass_on(0)
+        activate(-side)
+        pass_on(-side)
+        first_peaks()
+        loads[4].wait()
+        second_conv([-1, 0, 1], True, False)
 
     @pl.when(takes)
     def _():
-        hand_on().wait_recv()
-        second_part(past, True)
-
-    block = lat[...].astype(F32).reshape(width, C) + shifted_sum(acc[0, 0], acc[1, 0], acc[2, 0])
+        relay(REACH).wait_recv()
+        contribute(hist, True)
+        meet()
+        await_row(-2)
+        await_row(side)
+        await_row(2)
+        beside(rows_in, side, False)
+        await_row(-side)
+        beside(rows_in, -side, False)
+        loads[4].wait()
+        first_peaks()
+        await_past(-2)
+        await_past(side)
+        await_past(2)
+        beside(hist, side, True)
+        activate(side)
+        second_conv([side], True, True)
+        await_past(-side)
+        beside(hist, -side, True)
+        activate(0)
+        activate(-side)
+        second_conv([0, -side], False, True)
+
+    block = lat[...].astype(F32).reshape(width, C) + shifted_sum(mix[0], mix[1], mix[2])
     block = block.astype(BF16)
     wide_block = block.astype(F32)
     merged[1] = packed(wide_block, cols)
-    put_peak(pk2_send, 0, peak_of(wide_block))
+    pk2_send[...] = jnp.concatenate([pk_second[...], two_rows(peak_of(wide_block))], axis=0).astype(BF16)
     send_peaks(*last)
 
     def edge_copy(d):
@@ -376,13 +431,10 @@
         for j in range(2):
             dec_ref[f, j] = wide[j * C2 : (j + 1) * C2, f * 2 * cols : (f + 1) * 2 * cols]
 
-    best = take_peaks(*early)
-    for i in range(2):
+    best = jnp.concatenate([take_peaks(*early), take_peaks(*last)], axis=0)
+    for i in range(3):
         peaks_ref[i : i + 1, 0:LANES] = best[2 * i : 2 * i + 1, :]
         peaks_ref[i : i + 1, LANES:C] = best[2 * i + 1 : 2 * i + 2, 0 : C - LANES]
-    best = take_peaks(*last)
-    peaks_ref[2:3, 0:LANES] = best[0:1, :]
-    peaks_ref[2:3, LANES:C] = best[1:2, 0 : C - LANES]
 
     end_peaks(*early)
     end_peaks(*last)
@@ -395,7 +447,8 @@
     def _():
         for d in (0, 1, -1, 2, -2):
             pl.when(there(d))(lambda d=d: relay(REACH + d).wait_send())
-        hand_on().wait_send()
+        for o in (-1, 0, 1):
+            hand_on(o).wait_send()
 
 
 def per_device(latent, gain_first, conv_first, gain_second, conv_second, conv_up):
@@ -427,23 +480,25 @@
             pltpu.VMEM((span, 3, cols, LANES), BF16),
             pltpu.VMEM((span, 3, cols, LANES), BF16),
             pltpu.VMEM((3, 3, width, C), F32),
+            pltpu.VMEM((3, width, C), F32),
             pltpu.VMEM((3, 3, cols, LANES), BF16),
             pltpu.VMEM((3, 3, cols, LANES), BF16),
             pltpu.VMEM((taps, depth, C), BF16),
             pltpu.VMEM((taps, depth, C), BF16),
             pltpu.VMEM((9 * C2, C), BF16),
             pltpu.VMEM((3, 3, cols, LANES), BF16),
-            pltpu.VMEM((4, LANES), F32),
-            pltpu.VMEM((n, 4, LANES), F32),
+            pltpu.VMEM((2, LANES), BF16),
+            pltpu.VMEM((n, 2, LANES), BF16),
+            pltpu.VMEM((4, LANES), BF16),
+            pltpu.VMEM((n, 4, LANES), BF16),
             pltpu.VMEM((2, LANES), F32),
-            pltpu.VMEM((n, 2, LANES), F32),
             dma((6,)),
             dma((span,)),
             dma((span,)),
             dma((span,)),
             dma((span,)),
-            dma,
-            dma,
+            dma((3,)),
+            dma((3,)),
             dma((3,)),
             dma((3,)),
             dma((n,)),

time: 19 us -> 18 us (0.947)
  Pallas kernels: 18.2 us -> 17.2 us
    pallas_call x1, Pallas kernels: 17.6 us -> 16.5 us  [per_device(): pl.pallas_call(functools.partial(kernel, R, T), out_shape=(pltpu.VMEM((fr...]
where the time goes in v2:
time: 18 us; the launch traced here: 17.8 us
  Pallas kernels  17.2 us (96%)
  between operations  0.64 us (4%)
    pallas_call x1, Pallas kernels, per_device(): pl.pallas_call(functools.partial(kernel, R, T), out_shape=(pltpu.VMEM((fr...  16.5 us
    pallas_call x1, Pallas kernels, per_device(): pl.pallas_call(finish, out_shape=(jax.ShapeDtypeStruct(decoded.shape, BF1...  0.66 us

profile of v2, /device:TPU:0, one launch (start us, length us, event | category | flops | bytes accessed | tf_op | source)
XLA Modules:
  0.0 17.8 jit_solution(1063486507865939901)
XLA Ops:
  0.6 16.5 %shard_map.77 = (bf16[2,2,96,128]{3,2,1,0:T(8,128)(2,1)S(1)}, f32[3,192]{1,0:T(4,128)S(1)}) custom-call(bf16[2,64,192]{2,1,0:T(8,128)(2,1)} %bitcast.7, bf16[192]{0:T(256)(128)(2,1)} %g1_hbm.1, bf16[27,192,192]{2,1,0:T(8,128)(2,1)} %bitcast.4, bf16[192]{0:T(256)(128)(2,1)} %g2_hbm.1, bf16[27,192,192]{2,1,0:T(8,128)(2,1)} %bitcast.5, bf16[864,192]{1,0:T(8,128)(2,1)} %bitcast.6), custom_call_target="tpu_custom_call" | custom-call | tf_op jit(solution)/shard_map/pallas_call | solution.py:468
  17.1 0.7 %shard_map.78 = (bf16[2,2,96,128]{3,2,1,0:T(8,128)(2,1)}, f32[3,192]{1,0:T(4,128)}) custom-call(bf16[2,2,96,128]{3,2,1,0:T(8,128)(2,1)S(1)} %get-tuple-element.4.dec_in, f32[3,192]{1,0:T(4,128)S(1)} %get-tuple-element.5.peaks_in), custom_call_target="tpu_custom_call" | custom-call | tf_op jit(solution)/shard_map/pallas_call | solution.py:520

commit v3 on v2

--- a/solution.py
+++ b/solution.py
@@ -12,6 +12,10 @@
 F32 = jnp.float32
 REACH = 2
 LANES = 128
+
+
+def stages_of(R):
+    return [REACH << i for i in range(R.bit_length()) if (REACH << i) < R - 1]
 
 
 def normed_silu(values, gain):
@@ -136,16 +140,17 @@
     def row_copy(d):
         slot = REACH - d
         return pltpu.make_async_remote_copy(
-            src_ref=rows_in.at[REACH], dst_ref=rows_in.at[slot], send_sem=x1_send.at[slot],
-            recv_sem=x1_recv.at[slot], device_id={"rows": r + d}, device_id_type=MESH,
-        )
-
-    for d in (-side, side, 2 * side, -2 * side):
+            src_ref=rows_in.at[REACH], dst_ref=rows_in.at[slot], send_sem=x1_send,
+            recv_sem=x1_recv.at[slot - jnp.where(slot > REACH, 1, 0)],
+            device_id={"rows": r + d}, device_id_type=MESH,
+        )
+
+    for d in (side, 2 * side, -2 * side, -side):
         pl.when(there(d))(lambda d=d: row_copy(d).start())
 
     def relay(slot):
         return pltpu.make_async_remote_copy(
-            src_ref=rows_in.at[slot], dst_ref=hist.at[slot], send_sem=rl_send.at[slot],
+            src_ref=rows_in.at[slot], dst_ref=hist.at[slot], send_sem=rl_send,
             recv_sem=rl_recv.at[slot], device_id={"tm": t + 1}, device_id_type=MESH,
         )
 
@@ -153,7 +158,7 @@
     takes = t > 0
     pl.when(gives)(lambda: relay(REACH).start())
 
-    stages = [REACH << i for i in range(R.bit_length()) if (REACH << i) < R - 1]
+    stages = stages_of(R)
 
     def tell(i):
         for way, d in enumerate((stages[i], -stages[i])):
@@ -249,46 +254,43 @@
         at = 1 + o
         return pltpu.make_async_remote_copy(
             src_ref=second.at[at], dst_ref=past.at[at],
-            send_sem=s_send.at[at], recv_sem=s_recv.at[at], device_id={"tm": t + 1}, device_id_type=MESH,
+            send_sem=s_send, recv_sem=s_recv, device_id={"tm": t + 1}, device_id_type=MESH,
         )
 
     loads[2].wait()
     gain2 = g2[...].astype(F32).reshape(1, C)
 
-    def second_conv(offsets, fresh, has_past):
-        rows = [1 + o for o in offsets]
-
+    def handed():
+        return pltpu.make_async_remote_copy(
+            src_ref=second, dst_ref=past, send_sem=s_send, recv_sem=s_recv,
+            device_id={"tm": t + 1}, device_id_type=MESH,
+        )
+
+    def second_conv(has_past):
         def frames_at(source):
-            pieces = [frames_of(source.at[j]) for j in rows]
+            pieces = [frames_of(source.at[j]) for j in range(3)]
             return [jnp.concatenate([piece[f] for piece in pieces], axis=1) for f in range(2)]
 
         def taps_at(i, k):
-            return [w2[(i * 3 + j) * 3 + k] for j in rows]
-
-        def add(k, part, value):
-            if fresh:
-                mix[k, part] = value
-            else:
-                mix[k, part] += value
+            return [w2[(i * 3 + j) * 3 + k] for j in range(3)]
 
         f0, f1 = frames_at(second)
         if has_past:
-            for o in offsets:
-                hand_on(o).wait_recv()
+            handed().wait_recv()
             h0, h1 = frames_at(past)
             early = jnp.concatenate([h0, h1, f0], axis=1)
             late = jnp.concatenate([h1, f0, f1], axis=1)
             lhs = jnp.concatenate([early, late], axis=0)
             for k in range(3):
                 taps = [tap for i in range(3) for tap in taps_at(i, k)]
-                add(k, slice(0, width), dot(lhs, jnp.concatenate(taps, axis=0)))
+                mix[k] = dot(lhs, jnp.concatenate(taps, axis=0))
         else:
             both = jnp.concatenate([f0, f1], axis=0)
             for k in range(3):
                 main = dot(both, jnp.concatenate(taps_at(2, k), axis=0))
                 extra = dot(f0, jnp.concatenate(taps_at(1, k), axis=0))
-                add(k, slice(0, cols), main[0:cols])
-                add(k, slice(cols, width), main[cols:] + extra)
+                mix[k, 0:cols] = main[0:cols]
+                mix[k, cols:] = main[cols:] + extra
 
     def meet():
         for i in range(1, len(stages)):
@@ -302,33 +304,33 @@
         p = jnp.where(2 * r >= R, i, n - 2 - i)
         return jnp.where(p >= me, p + 1, p)
 
-    def peak_copy(src, dst, ssem, rsem, peer, owner):
-        return pltpu.make_async_remote_copy(
-            src_ref=src, dst_ref=dst.at[owner], send_sem=ssem.at[peer], recv_sem=rsem.at[owner],
+    def peak_copy(src, dst, ssem, rsem, peer):
+        return pltpu.make_async_remote_copy(
+            src_ref=src, dst_ref=dst.at[me - jnp.where(me > peer, 1, 0)], send_sem=ssem, recv_sem=rsem,
             device_id={"rows": peer // T, "tm": lax.rem(peer, T)}, device_id_type=MESH,
         )
 
     def send_peaks(src, dst, ssem, rsem):
         def step(i, carry):
-            peak_copy(src, dst, ssem, rsem, peer_of(i), me).start()
+            peak_copy(src, dst, ssem, rsem, peer_of(i)).start()
             return carry
 
         lax.fori_loop(0, n - 1, step, 0, unroll=n <= 16)
 
-    def take_peaks(src, dst, ssem, rsem):
+    def all_peaks(src, dst, ssem, rsem):
+        return pltpu.make_async_remote_copy(
+            src_ref=dst, dst_ref=dst, send_sem=ssem, recv_sem=rsem,
+            device_id={"rows": r, "tm": lax.rem(t + 1, T)}, device_id_type=MESH,
+        )
+
+    def take_peaks(*refs):
+        src, dst = refs[0:2]
+        all_peaks(*refs).wait_recv()
+
         def step(i, best):
-            peer = peer_of(n - 2 - i)
-            peak_copy(src, dst, ssem, rsem, peer, peer).wait_recv()
-            return jnp.maximum(best, dst[peer].astype(F32))
+            return jnp.maximum(best, dst[i].astype(F32))
 
         return lax.fori_loop(0, n - 1, step, src[...].astype(F32), unroll=n <= 16)
-
-    def end_peaks(src, dst, ssem, rsem):
-        def step(i, carry):
-            peak_copy(src, dst, ssem, rsem, peer_of(i), me).wait_send()
-            return carry
-
-        lax.fori_loop(0, n - 1, step, 0, unroll=n <= 16)
 
     early = (pk1_send, pk1_recv, pk1_ssem, pk1_rsem)
     last = (pk2_send, pk2_recv, pk2_ssem, pk2_rsem)
@@ -358,7 +360,7 @@
         pass_on(-side)
         first_peaks()
         loads[4].wait()
-        second_conv([-1, 0, 1], True, False)
+        second_conv(False)
 
     @pl.when(takes)
     def _():
@@ -377,13 +379,12 @@
         await_past(side)
         await_past(2)
         beside(hist, side, True)
-        activate(side)
-        second_conv([side], True, True)
         await_past(-side)
         beside(hist, -side, True)
+        activate(side)
         activate(0)
         activate(-side)
-        second_conv([0, -side], False, True)
+        second_conv(True)
 
     block = lat[...].astype(F32).reshape(width, C) + shifted_sum(mix[0], mix[1], mix[2])
     block = block.astype(BF16)
@@ -395,11 +396,11 @@
     def edge_copy(d):
         slot = 1 - d
         return pltpu.make_async_remote_copy(
-            src_ref=merged.at[1], dst_ref=merged.at[slot], send_sem=x3_send.at[slot],
-            recv_sem=x3_recv.at[slot], device_id={"rows": r + d}, device_id_type=MESH,
-        )
-
-    for d in (-side, side):
+            src_ref=merged.at[1], dst_ref=merged.at[slot], send_sem=x3_send,
+            recv_sem=x3_recv.at[slot // 2], device_id={"rows": r + d}, device_id_type=MESH,
+        )
+
+    for d in (side, -side):
         pl.when(there(d))(lambda d=d: edge_copy(d).start())
 
     loads[5].wait()
@@ -436,19 +437,25 @@
         peaks_ref[i : i + 1, 0:LANES] = best[2 * i : 2 * i + 1, :]
         peaks_ref[i : i + 1, LANES:C] = best[2 * i + 1 : 2 * i + 2, 0 : C - LANES]
 
-    end_peaks(*early)
-    end_peaks(*last)
-    for d in (1, -1, 2, -2):
-        pl.when(there(d))(lambda d=d: row_copy(d).wait_send())
-    for d in (1, -1):
-        pl.when(there(d))(lambda d=d: edge_copy(d).wait_send())
+    all_peaks(*early).wait_send()
+    all_peaks(*last).wait_send()
+
+    def sent(ref, sem, count, most):
+        for c in range(1, most + 1):
+            pl.when(count == c)(
+                lambda c=c: pltpu.make_async_remote_copy(
+                    src_ref=ref.at[pl.ds(0, c)], dst_ref=ref.at[pl.ds(0, c)], send_sem=sem, recv_sem=sem,
+                    device_id={"rows": r, "tm": lax.rem(t + 1, T)}, device_id_type=MESH,
+                ).wait_send()
+            )
+
+    sent(rows_in, x1_send, rows_near - 1, 2 * REACH)
+    sent(merged, x3_send, jnp.minimum(r, 1) + jnp.minimum(R - 1 - r, 1), 2)
 
     @pl.when(gives)
     def _():
-        for d in (0, 1, -1, 2, -2):
-            pl.when(there(d))(lambda d=d: relay(REACH + d).wait_send())
-        for o in (-1, 0, 1):
-            hand_on(o).wait_send()
+        sent(rows_in, rl_send, rows_near, 2 * REACH + 1)
+        handed().wait_send()
 
 
 def per_device(latent, gain_first, conv_first, gain_second, conv_second, conv_up):
@@ -488,24 +495,24 @@
             pltpu.VMEM((9 * C2, C), BF16),
             pltpu.VMEM((3, 3, cols, LANES), BF16),
             pltpu.VMEM((2, LANES), BF16),
-            pltpu.VMEM((n, 2, LANES), BF16),
+            pltpu.VMEM((n - 1, 2, LANES), BF16),
             pltpu.VMEM((4, LANES), BF16),
-            pltpu.VMEM((n, 4, LANES), BF16),
+            pltpu.VMEM((n - 1, 4, LANES), BF16),
             pltpu.VMEM((2, LANES), F32),
             dma((6,)),
+            dma,
+            dma((span - 1,)),
+            dma,
             dma((span,)),
-            dma((span,)),
-            dma((span,)),
-            dma((span,)),
-            dma((3,)),
-            dma((3,)),
-            dma((3,)),
-            dma((3,)),
-            dma((n,)),
-            dma((n,)),
-            dma((n,)),
-            dma((n,)),
-            pltpu.SemaphoreType.REGULAR((R.bit_length(), 2)),
+            dma,
+            dma,
+            dma,
+            dma((2,)),
+            dma,
+            dma,
+            dma,
+            dma,
+            pltpu.SemaphoreType.REGULAR((max(1, len(stages_of(R))), 2)),
             pltpu.VMEM((2 * width, 2 * width), BF16),
         ],
         compiler_params=pltpu.CompilerParams(collective_id=0, has_side_effects=True, vmem_limit_bytes=54 * 2**20),

time: 18 us -> 17 us (0.944)
  Pallas kernels: 17.2 us -> 16.2 us
    pallas_call x1, Pallas kernels: 16.5 us -> 15.5 us  [per_device(): pl.pallas_call(functools.partial(kernel, R, T), out_shape=(pltpu.VMEM((fr...]
where the time goes in v3:
time: 17 us; the launch traced here: 16.8 us
  Pallas kernels  16.2 us (95%)
  between operations  0.64 us (4%)
    pallas_call x1, Pallas kernels, per_device(): pl.pallas_call(functools.partial(kernel, R, T), out_shape=(pltpu.VMEM((fr...  15.5 us
    pallas_call x1, Pallas kernels, per_device(): pl.pallas_call(finish, out_shape=(jax.ShapeDtypeStruct(decoded.shape, BF1...  0.66 us

profile of v3, /device:TPU:0, one launch (start us, length us, event | category | flops | bytes accessed | tf_op | source)
XLA Modules:
  0.0 16.8 jit_solution(8091757613310819301)
XLA Ops:
  0.6 15.5 %shard_map.77 = (bf16[2,2,96,128]{3,2,1,0:T(8,128)(2,1)S(1)}, f32[3,192]{1,0:T(4,128)S(1)}) custom-call(bf16[2,64,192]{2,1,0:T(8,128)(2,1)} %bitcast.7, bf16[192]{0:T(256)(128)(2,1)} %g1_hbm.1, bf16[27,192,192]{2,1,0:T(8,128)(2,1)} %bitcast.4, bf16[192]{0:T(256)(128)(2,1)} %g2_hbm.1, bf16[27,192,192]{2,1,0:T(8,128)(2,1)} %bitcast.5, bf16[864,192]{1,0:T(8,128)(2,1)} %bitcast.6), custom_call_target="tpu_custom_call" | custom-call | tf_op jit(solution)/shard_map/pallas_call | solution.py:475
  16.2 0.7 %shard_map.78 = (bf16[2,2,96,128]{3,2,1,0:T(8,128)(2,1)}, f32[3,192]{1,0:T(4,128)}) custom-call(bf16[2,2,96,128]{3,2,1,0:T(8,128)(2,1)S(1)} %get-tuple-element.4.dec_in, f32[3,192]{1,0:T(4,128)S(1)} %get-tuple-element.5.peaks_in), custom_call_target="tpu_custom_call" | custom-call | tf_op jit(solution)/shard_map/pallas_call | solution.py:527

commit v4 on v3

--- a/solution.py
+++ b/solution.py
@@ -61,10 +61,10 @@
 
 def kernel(
     R, T, lat_hbm, g1_hbm, w1_hbm, g2_hbm, w2_hbm, up_hbm, dec_ref, peaks_ref,
-    lat, g1, g2, rows_in, hist, acc, mix, second, past, w1, w2, up, merged,
-    pk1_send, pk1_recv, pk2_send, pk2_recv, pk_second,
+    lat, g1, g2, rows_in, hist, acc, mix, gift, gift_out, base, second, w1, w2, up, merged,
+    pk_send, pk_recv, pk_first, pk_second,
     load_sem, x1_send, x1_recv, rl_send, rl_recv, s_send, s_recv, x3_send, x3_recv,
-    pk1_ssem, pk1_rsem, pk2_ssem, pk2_rsem, known, spread,
+    pk_ssem, pk_rsem, known, spread,
 ):
     r = lax.axis_index("rows")
     t = lax.axis_index("tm")
@@ -113,8 +113,12 @@
         def _(d=d):
             rows_in[REACH + d] = jnp.zeros_like(rows_in[REACH + d])
             hist[REACH + d] = jnp.zeros_like(hist[REACH + d])
-            if abs(d) == 1:
-                second[1 + d] = jnp.zeros_like(second[1 + d])
+
+    second[...] = jnp.zeros_like(second)
+
+    @pl.when(t == 0)
+    def _():
+        gift[...] = jnp.zeros_like(gift)
 
     pad = w1.shape[1] - C
     w1[:, C:, :] = jnp.zeros((w1.shape[0], pad, C), BF16)
@@ -179,7 +183,7 @@
         rest = jnp.concatenate([row[:, LANES:C], jnp.zeros((1, 2 * LANES - C), F32)], axis=1)
         return jnp.concatenate([row[:, 0:LANES], rest], axis=0)
 
-    pk1_send[...] = two_rows(peak_of(own_first.astype(BF16).astype(F32))).astype(BF16)
+    pk_first[...] = two_rows(peak_of(own_first.astype(BF16).astype(F32)))
 
     def contribute(source, past_frames):
         f0, f1 = frames_of(source.at[REACH])
@@ -236,109 +240,80 @@
         right = jnp.where(lane0 == cols - 1, 0.0, pltpu.roll(right, width - 1, 0))
         return left + middle + right
 
-    def activate(o):
-        if isinstance(o, int):
-            activate_row(o)
+    def activate(slot):
+        o = (side, 0, -side)[slot]
+        if slot == 1:
+            activate_row(slot, o)
         else:
-            pl.when(there(o))(lambda: activate_row(o))
-
-    def activate_row(o):
+            pl.when(there(o))(lambda: activate_row(slot, o))
+
+    def activate_row(slot, o):
         at = 1 + o
         hidden = shifted_sum(acc[0, at], acc[1, at], acc[2, at]).astype(BF16).astype(F32)
-        values = normed_silu(hidden, gain2)
-        if isinstance(o, int):
-            pk_second[...] = two_rows(peak_of(values.astype(BF16).astype(F32)))
-        second[at] = packed(values, cols)
-
-    def hand_on(o):
-        at = 1 + o
+        values = normed_silu(hidden, gain2).astype(BF16)
+        if slot == 1:
+            pk_second[...] = two_rows(peak_of(values.astype(F32)))
+        second[slot, :, 0:C] = values
+
+    def gift_copy():
         return pltpu.make_async_remote_copy(
-            src_ref=second.at[at], dst_ref=past.at[at],
-            send_sem=s_send, recv_sem=s_recv, device_id={"tm": t + 1}, device_id_type=MESH,
+            src_ref=gift_out, dst_ref=gift, send_sem=s_send, recv_sem=s_recv,
+            device_id={"tm": t + 1}, device_id_type=MESH,
         )
 
     loads[2].wait()
     gain2 = g2[...].astype(F32).reshape(1, C)
 
-    def handed():
-        return pltpu.make_async_remote_copy(
-            src_ref=second, dst_ref=past, send_sem=s_send, recv_sem=s_recv,
-            device_id={"tm": t + 1}, device_id_type=MESH,
-        )
-
-    def second_conv(has_past):
-        def frames_at(source):
-            pieces = [frames_of(source.at[j]) for j in range(3)]
-            return [jnp.concatenate([piece[f] for piece in pieces], axis=1) for f in range(2)]
+    def second_conv(past_frames):
+        rows = [second[slot] for slot in range(3)]
+        both = jnp.concatenate(rows, axis=1)
+        one = jnp.concatenate([row[cols:] if past_frames else row[0:cols] for row in rows], axis=1)
 
         def taps_at(i, k):
-            return [w2[(i * 3 + j) * 3 + k] for j in range(3)]
-
-        f0, f1 = frames_at(second)
-        if has_past:
-            handed().wait_recv()
-            h0, h1 = frames_at(past)
-            early = jnp.concatenate([h0, h1, f0], axis=1)
-            late = jnp.concatenate([h1, f0, f1], axis=1)
-            lhs = jnp.concatenate([early, late], axis=0)
-            for k in range(3):
-                taps = [tap for i in range(3) for tap in taps_at(i, k)]
-                mix[k] = dot(lhs, jnp.concatenate(taps, axis=0))
+            return jnp.concatenate([w2[(i * 3 + 1 + o) * 3 + k] for o in (side, 0, -side)], axis=0)
+
+        sums = []
+        for k in range(3):
+            main = dot(both, taps_at(0 if past_frames else 2, k))
+            extra = dot(one, taps_at(1, k))
+            if past_frames:
+                sums.append(jnp.concatenate([main[0:cols] + extra, main[cols:]], axis=0))
+            else:
+                sums.append(jnp.concatenate([main[0:cols], main[cols:] + extra], axis=0))
+        if past_frames:
+            gift_out[...] = shifted_sum(*sums).astype(BF16)
         else:
-            both = jnp.concatenate([f0, f1], axis=0)
-            for k in range(3):
-                main = dot(both, jnp.concatenate(taps_at(2, k), axis=0))
-                extra = dot(f0, jnp.concatenate(taps_at(1, k), axis=0))
-                mix[k, 0:cols] = main[0:cols]
-                mix[k, cols:] = main[cols:] + extra
+            mix[...] = shifted_sum(*sums)
 
     def meet():
         for i in range(1, len(stages)):
             hear(i - 1)
             tell(i)
 
-    def pass_on(o):
-        pl.when(gives)(lambda: hand_on(o).start())
-
-    def peer_of(i):
-        p = jnp.where(2 * r >= R, i, n - 2 - i)
-        return jnp.where(p >= me, p + 1, p)
-
-    def peak_copy(src, dst, ssem, rsem, peer):
+    def peak_copy(peer):
         return pltpu.make_async_remote_copy(
-            src_ref=src, dst_ref=dst.at[me - jnp.where(me > peer, 1, 0)], send_sem=ssem, recv_sem=rsem,
+            src_ref=pk_send, dst_ref=pk_recv.at[me - jnp.where(me > peer, 1, 0)],
+            send_sem=pk_ssem, recv_sem=pk_rsem,
             device_id={"rows": peer // T, "tm": lax.rem(peer, T)}, device_id_type=MESH,
         )
 
-    def send_peaks(src, dst, ssem, rsem):
+    def send_peaks():
         def step(i, carry):
-            peak_copy(src, dst, ssem, rsem, peer_of(i)).start()
+            p = jnp.where(2 * r >= R, i, n - 2 - i)
+            peak_copy(jnp.where(p >= me, p + 1, p)).start()
             return carry
 
         lax.fori_loop(0, n - 1, step, 0, unroll=n <= 16)
 
-    def all_peaks(src, dst, ssem, rsem):
+    def all_peaks():
         return pltpu.make_async_remote_copy(
-            src_ref=dst, dst_ref=dst, send_sem=ssem, recv_sem=rsem,
+            src_ref=pk_recv, dst_ref=pk_recv, send_sem=pk_ssem, recv_sem=pk_rsem,
             device_id={"rows": r, "tm": lax.rem(t + 1, T)}, device_id_type=MESH,
         )
 
-    def take_peaks(*refs):
-        src, dst = refs[0:2]
-        all_peaks(*refs).wait_recv()
-
-        def step(i, best):
-            return jnp.maximum(best, dst[i].astype(F32))
-
-        return lax.fori_loop(0, n - 1, step, src[...].astype(F32), unroll=n <= 16)
-
-    early = (pk1_send, pk1_recv, pk1_ssem, pk1_rsem)
-    last = (pk2_send, pk2_recv, pk2_ssem, pk2_rsem)
-
-    def first_peaks():
+    def heard():
         if stages:
             hear(len(stages) - 1)
-        send_peaks(*early)
 
     def beside(source, s, past_frames):
         pl.when(there(s))(lambda: contribute_side(source, s, past_frames))
@@ -350,16 +325,18 @@
         await_row(side)
         await_row(2)
         beside(rows_in, side, False)
-        activate(side)
-        pass_on(side)
         await_row(-side)
+        activate(0)
         beside(rows_in, -side, False)
-        activate(0)
-        pass_on(0)
-        activate(-side)
-        pass_on(-side)
-        first_peaks()
+        activate(1)
+        activate(2)
         loads[4].wait()
+
+        @pl.when(gives)
+        def _():
+            second_conv(True)
+            gift_copy().start()
+
         second_conv(False)
 
     @pl.when(takes)
@@ -374,24 +351,27 @@
         await_row(-side)
         beside(rows_in, -side, False)
         loads[4].wait()
-        first_peaks()
+        heard()
         await_past(-2)
         await_past(side)
         await_past(2)
         beside(hist, side, True)
+        activate(0)
         await_past(-side)
         beside(hist, -side, True)
-        activate(side)
-        activate(0)
-        activate(-side)
-        second_conv(True)
-
-    block = lat[...].astype(F32).reshape(width, C) + shifted_sum(mix[0], mix[1], mix[2])
+        activate(1)
+        activate(2)
+        second_conv(False)
+        gift_copy().wait_recv()
+
+    block = lat[...].astype(F32).reshape(width, C) + mix[...] + gift[...].astype(F32)
     block = block.astype(BF16)
     wide_block = block.astype(F32)
     merged[1] = packed(wide_block, cols)
-    pk2_send[...] = jnp.concatenate([pk_second[...], two_rows(peak_of(wide_block))], axis=0).astype(BF16)
-    send_peaks(*last)
+    peaks = jnp.concatenate([pk_first[...], pk_second[...], two_rows(peak_of(wide_block))], axis=0)
+    pk_send[...] = peaks.astype(BF16)
+    pl.when(jnp.logical_not(takes))(heard)
+    send_peaks()
 
     def edge_copy(d):
         slot = 1 - d
@@ -406,17 +386,8 @@
     loads[5].wait()
     C2 = dec_ref.shape[2]
     own = dot_nt(up[...], block).reshape(3, 3, C2, width)
-    upper = own[1] + own[2]
-    lower = own[0] + own[1]
-
-    def edge_row(slot):
-        f0, f1 = frames_of(merged.at[slot])
-        return jnp.concatenate([f0, f1], axis=0)[:, 0:C]
-
-    for d in (side, -side):
-        pl.when(there(d))(lambda d=d: edge_copy(-d).wait_recv())
-    upper = upper + dot_nt(up[0 : 3 * C2], edge_row(0)).reshape(3, C2, width)
-    lower = lower + dot_nt(up[6 * C2 :], edge_row(2)).reshape(3, C2, width)
+    base[0] = own[1] + own[2]
+    base[1] = own[0] + own[1]
     lane = lax.rem(lax.broadcasted_iota(jnp.int32, (C2, width), 1), cols)
 
     def columns(sums):
@@ -426,19 +397,28 @@
         odd = sums[0] + sums[1] + from_right
         return jnp.concatenate([even, odd], axis=1).astype(BF16)
 
-    narrow = jnp.concatenate([columns(upper), columns(lower)], axis=0)
-    wide = dot(narrow, spread[...]).astype(BF16)
-    for f in range(frames):
-        for j in range(2):
-            dec_ref[f, j] = wide[j * C2 : (j + 1) * C2, f * 2 * cols : (f + 1) * 2 * cols]
-
-    best = jnp.concatenate([take_peaks(*early), take_peaks(*last)], axis=0)
+    def decode_row(half):
+        f0, f1 = frames_of(merged.at[2 * half])
+        rows = jnp.concatenate([f0, f1], axis=0)[:, 0:C]
+        taps = up[half * 6 * C2 : (half * 6 + 3) * C2]
+        sums = base[half] + dot_nt(taps, rows).reshape(3, C2, width)
+        wide = dot(columns(sums), spread[...]).astype(BF16)
+        for f in range(frames):
+            dec_ref[f, half] = wide[:, f * 2 * cols : (f + 1) * 2 * cols]
+
+    for d in (-1, 1):
+        pl.when(there(d))(lambda d=d: edge_copy(-d).wait_recv())
+        decode_row((1 + d) // 2)
+
+    all_peaks().wait_recv()
+
+    def take_peak(i, best):
+        return jnp.maximum(best, pk_recv[i].astype(F32))
+
+    best = lax.fori_loop(0, n - 1, take_peak, peaks, unroll=n <= 16)
     for i in range(3):
         peaks_ref[i : i + 1, 0:LANES] = best[2 * i : 2 * i + 1, :]
         peaks_ref[i : i + 1, LANES:C] = best[2 * i + 1 : 2 * i + 2, 0 : C - LANES]
-
-    all_peaks(*early).wait_send()
-    all_peaks(*last).wait_send()
 
     def sent(ref, sem, count, most):
         for c in range(1, most + 1):
@@ -455,7 +435,9 @@
     @pl.when(gives)
     def _():
         sent(rows_in, rl_send, rows_near, 2 * REACH + 1)
-        handed().wait_send()
+        gift_copy().wait_send()
+
+    all_peaks().wait_send()
 
 
 def per_device(latent, gain_first, conv_first, gain_second, conv_second, conv_up):
@@ -487,17 +469,18 @@
             pltpu.VMEM((span, 3, cols, LANES), BF16),
             pltpu.VMEM((span, 3, cols, LANES), BF16),
             pltpu.VMEM((3, 3, width, C), F32),
-            pltpu.VMEM((3, width, C), F32),
-            pltpu.VMEM((3, 3, cols, LANES), BF16),
-            pltpu.VMEM((3, 3, cols, LANES), BF16),
+            pltpu.VMEM((width, C), F32),
+            pltpu.VMEM((width, C), BF16),
+            pltpu.VMEM((width, C), BF16),
+            pltpu.VMEM((2, 3, C2, width), F32),
+            pltpu.VMEM((3, width, depth), BF16),
             pltpu.VMEM((taps, depth, C), BF16),
             pltpu.VMEM((taps, depth, C), BF16),
             pltpu.VMEM((9 * C2, C), BF16),
             pltpu.VMEM((3, 3, cols, LANES), BF16),
-            pltpu.VMEM((2, LANES), BF16),
-            pltpu.VMEM((n - 1, 2, LANES), BF16),
-            pltpu.VMEM((4, LANES), BF16),
-            pltpu.VMEM((n - 1, 4, LANES), BF16),
+            pltpu.VMEM((6, LANES), BF16),
+            pltpu.VMEM((n - 1, 6, LANES), BF16),
+            pltpu.VMEM((2, LANES), F32),
             pltpu.VMEM((2, LANES), F32),
             dma((6,)),
             dma,
@@ -508,8 +491,6 @@
             dma,
             dma,
             dma((2,)),
-            dma,
-            dma,
             dma,
             dma,
             pltpu.SemaphoreType.REGULAR((max(1, len(stages_of(R))), 2)),

time: 17 us -> 16.7 us (0.982)
  Pallas kernels: 16.2 us -> 15.9 us
    pallas_call x1, Pallas kernels: 15.5 us -> 15.3 us  [per_device(): pl.pallas_call(functools.partial(kernel, R, T), out_shape=(pltpu.VMEM((fr...]
where the time goes in v4:
time: 16.7 us; the launch traced here: 16.6 us
  Pallas kernels  15.9 us (95%)
  between operations  0.64 us (4%)
    pallas_call x1, Pallas kernels, per_device(): pl.pallas_call(functools.partial(kernel, R, T), out_shape=(pltpu.VMEM((fr...  15.3 us
    pallas_call x1, Pallas kernels, per_device(): pl.pallas_call(finish, out_shape=(jax.ShapeDtypeStruct(decoded.shape, BF1...  0.66 us

profile of v4, /device:TPU:0, one launch (start us, length us, event | category | flops | bytes accessed | tf_op | source)
XLA Modules:
  0.0 16.6 jit_solution(12308731079541635410)
XLA Ops:
  0.6 15.3 %shard_map.77 = (bf16[2,2,96,128]{3,2,1,0:T(8,128)(2,1)S(1)}, f32[3,192]{1,0:T(4,128)S(1)}) custom-call(bf16[2,64,192]{2,1,0:T(8,128)(2,1)} %bitcast.7, bf16[192]{0:T(256)(128)(2,1)} %g1_hbm.1, bf16[27,192,192]{2,1,0:T(8,128)(2,1)} %bitcast.4, bf16[192]{0:T(256)(128)(2,1)} %g2_hbm.1, bf16[27,192,192]{2,1,0:T(8,128)(2,1)} %bitcast.5, bf16[864,192]{1,0:T(8,128)(2,1)} %bitcast.6), custom_call_target="tpu_custom_call" | custom-call | tf_op jit(solution)/shard_map/pallas_call | solution.py:457
  15.9 0.7 %shard_map.78 = (bf16[2,2,96,128]{3,2,1,0:T(8,128)(2,1)}, f32[3,192]{1,0:T(4,128)}) custom-call(bf16[2,2,96,128]{3,2,1,0:T(8,128)(2,1)S(1)} %get-tuple-element.4.dec_in, f32[3,192]{1,0:T(4,128)S(1)} %get-tuple-element.5.peaks_in), custom_call_target="tpu_custom_call" | custom-call | tf_op jit(solution)/shard_map/pallas_call | solution.py:508

commit v5 on v4

--- a/solution.py
+++ b/solution.py
@@ -62,9 +62,9 @@
 def kernel(
     R, T, lat_hbm, g1_hbm, w1_hbm, g2_hbm, w2_hbm, up_hbm, dec_ref, peaks_ref,
     lat, g1, g2, rows_in, hist, acc, mix, gift, gift_out, base, second, w1, w2, up, merged,
-    pk_send, pk_recv, pk_first, pk_second,
+    pk_send, pk_recv, pk_past, pk_first, pk_second,
     load_sem, x1_send, x1_recv, rl_send, rl_recv, s_send, s_recv, x3_send, x3_recv,
-    pk_ssem, pk_rsem, known, spread,
+    pk_ssem, pk_rsem, pp_rsem, known, spread,
 ):
     r = lax.axis_index("rows")
     t = lax.axis_index("tm")
@@ -290,10 +290,15 @@
             hear(i - 1)
             tell(i)
 
+    last_core = t == T - 1
+    alone = 2 * r >= R
+    alone_rows = R - (R + 1) // 2
+    sources = R + alone_rows * (T - 1)
+    slot = jnp.where(last_core, r, R + (r - (R - alone_rows)) * (T - 1) + t)
+
     def peak_copy(peer):
         return pltpu.make_async_remote_copy(
-            src_ref=pk_send, dst_ref=pk_recv.at[me - jnp.where(me > peer, 1, 0)],
-            send_sem=pk_ssem, recv_sem=pk_rsem,
+            src_ref=pk_send, dst_ref=pk_recv.at[slot], send_sem=pk_ssem, recv_sem=pk_rsem,
             device_id={"rows": peer // T, "tm": lax.rem(peer, T)}, device_id_type=MESH,
         )
 
@@ -305,11 +310,20 @@
 
         lax.fori_loop(0, n - 1, step, 0, unroll=n <= 16)
 
-    def all_peaks():
-        return pltpu.make_async_remote_copy(
-            src_ref=pk_recv, dst_ref=pk_recv, send_sem=pk_ssem, recv_sem=pk_rsem,
+    def pass_peaks():
+        return pltpu.make_async_remote_copy(
+            src_ref=pk_send, dst_ref=pk_past, send_sem=pk_ssem, recv_sem=pp_rsem,
+            device_id={"tm": t + 1}, device_id_type=MESH,
+        )
+
+    def peaks_of(count):
+        return pltpu.make_async_remote_copy(
+            src_ref=pk_recv.at[pl.ds(0, count)], dst_ref=pk_recv.at[pl.ds(0, count)],
+            send_sem=pk_ssem, recv_sem=pk_rsem,
             device_id={"rows": r, "tm": lax.rem(t + 1, T)}, device_id_type=MESH,
         )
+
+    shares = jnp.logical_or(last_core, alone)
 
     def heard():
         if stages:
@@ -369,19 +383,45 @@
     wide_block = block.astype(F32)
     merged[1] = packed(wide_block, cols)
     peaks = jnp.concatenate([pk_first[...], pk_second[...], two_rows(peak_of(wide_block))], axis=0)
+    def edge_copy(d):
+        slot = 1 - d
+        return pltpu.make_async_remote_copy(
+            src_ref=merged.at[1], dst_ref=merged.at[slot], send_sem=x3_send,
+            recv_sem=x3_recv.at[slot // 2], device_id={"rows": r + d}, device_id_type=MESH,
+        )
+
+    def send_edges():
+        for d in (side, -side):
+            pl.when(there(d))(lambda d=d: edge_copy(d).start())
+
+    def with_past():
+        @pl.when(jnp.logical_and(takes, jnp.logical_not(alone)))
+        def _():
+            pass_peaks().wait_recv()
+            pk_send[...] = jnp.maximum(pk_send[...].astype(F32), pk_past[...].astype(F32)).astype(BF16)
+
     pk_send[...] = peaks.astype(BF16)
     pl.when(jnp.logical_not(takes))(heard)
-    send_peaks()
-
-    def edge_copy(d):
-        slot = 1 - d
-        return pltpu.make_async_remote_copy(
-            src_ref=merged.at[1], dst_ref=merged.at[slot], send_sem=x3_send,
-            recv_sem=x3_recv.at[slot // 2], device_id={"rows": r + d}, device_id_type=MESH,
-        )
-
-    for d in (side, -side):
-        pl.when(there(d))(lambda d=d: edge_copy(d).start())
+    low = jnp.logical_and(2 * r < R, takes)
+
+    @pl.when(low)
+    def _():
+        send_edges()
+
+    with_past()
+
+    @pl.when(shares)
+    def _():
+        pk_recv[slot] = pk_send[...]
+        send_peaks()
+
+    @pl.when(jnp.logical_not(shares))
+    def _():
+        pass_peaks().start()
+
+    @pl.when(jnp.logical_not(low))
+    def _():
+        send_edges()
 
     loads[5].wait()
     C2 = dec_ref.shape[2]
@@ -410,12 +450,13 @@
         pl.when(there(d))(lambda d=d: edge_copy(-d).wait_recv())
         decode_row((1 + d) // 2)
 
-    all_peaks().wait_recv()
+    pl.when(shares)(lambda: peaks_of(sources - 1).wait_recv())
+    pl.when(jnp.logical_not(shares))(lambda: peaks_of(sources).wait_recv())
 
     def take_peak(i, best):
         return jnp.maximum(best, pk_recv[i].astype(F32))
 
-    best = lax.fori_loop(0, n - 1, take_peak, peaks, unroll=n <= 16)
+    best = lax.fori_loop(1, sources, take_peak, pk_recv[0].astype(F32), unroll=n <= 16)
     for i in range(3):
         peaks_ref[i : i + 1, 0:LANES] = best[2 * i : 2 * i + 1, :]
         peaks_ref[i : i + 1, LANES:C] = best[2 * i + 1 : 2 * i + 2, 0 : C - LANES]
@@ -437,7 +478,8 @@
         sent(rows_in, rl_send, rows_near, 2 * REACH + 1)
         gift_copy().wait_send()
 
-    all_peaks().wait_send()
+    pl.when(shares)(lambda: peaks_of(n - 1).wait_send())
+    pl.when(jnp.logical_not(shares))(lambda: pass_peaks().wait_send())
 
 
 def per_device(latent, gain_first, conv_first, gain_second, conv_second, conv_up):
@@ -479,7 +521,8 @@
             pltpu.VMEM((9 * C2, C), BF16),
             pltpu.VMEM((3, 3, cols, LANES), BF16),
             pltpu.VMEM((6, LANES), BF16),
-            pltpu.VMEM((n - 1, 6, LANES), BF16),
+            pltpu.VMEM((n + R, 6, LANES), BF16),
+            pltpu.VMEM((6, LANES), BF16),
             pltpu.VMEM((2, LANES), F32),
             pltpu.VMEM((2, LANES), F32),
             dma((6,)),
@@ -491,6 +534,7 @@
             dma,
             dma,
             dma((2,)),
+            dma,
             dma,
             dma,
             pltpu.SemaphoreType.REGULAR((max(1, len(stages_of(R))), 2)),

time: 16.7 us -> 16.7 us (level)
  no operation moved by 1% of the time
where the time goes in v5:
time: 16.7 us; the launch traced here: 16.6 us
  Pallas kernels  15.9 us (95%)
  between operations  0.64 us (4%)
    pallas_call x1, Pallas kernels, per_device(): pl.pallas_call(functools.partial(kernel, R, T), out_shape=(pltpu.VMEM((fr...  15.3 us
    pallas_call x1, Pallas kernels, per_device(): pl.pallas_call(finish, out_shape=(jax.ShapeDtypeStruct(decoded.shape, BF1...  0.66 us

profile of v5, /device:TPU:0, one launch (start us, length us, event | category | flops | bytes accessed | tf_op | source)
XLA Modules:
  0.0 16.6 jit_solution(17217963869432585769)
XLA Ops:
  0.6 15.3 %shard_map.77 = (bf16[2,2,96,128]{3,2,1,0:T(8,128)(2,1)S(1)}, f32[3,192]{1,0:T(4,128)S(1)}) custom-call(bf16[2,64,192]{2,1,0:T(8,128)(2,1)} %bitcast.7, bf16[192]{0:T(256)(128)(2,1)} %g1_hbm.1, bf16[27,192,192]{2,1,0:T(8,128)(2,1)} %bitcast.4, bf16[192]{0:T(256)(128)(2,1)} %g2_hbm.1, bf16[27,192,192]{2,1,0:T(8,128)(2,1)} %bitcast.5, bf16[864,192]{1,0:T(8,128)(2,1)} %bitcast.6), custom_call_target="tpu_custom_call" | custom-call | tf_op jit(solution)/shard_map/pallas_call | solution.py:499
  15.9 0.7 %shard_map.78 = (bf16[2,2,96,128]{3,2,1,0:T(8,128)(2,1)}, f32[3,192]{1,0:T(4,128)}) custom-call(bf16[2,2,96,128]{3,2,1,0:T(8,128)(2,1)S(1)} %get-tuple-element.4.dec_in, f32[3,192]{1,0:T(4,128)S(1)} %get-tuple-element.5.peaks_in), custom_call_target="tpu_custom_call" | custom-call | tf_op jit(solution)/shard_map/pallas_call | solution.py:552
